TPU v7x, 256 devices: a whole 4x4x8 slice. The times are simulated.
256 devices in a mesh: chan: 8 (over z), tm: 32 (over x, y, core).
Axes of the slice: x: 4, y: 4, z: 8, core: 2. Of those that a mesh axis runs over, the one named last changes fastest.
Arguments:
- trajectory: float32 [2048, 8, 4096], P('tm', None, 'chan'), may hold values from -40 to 40
- initial: float32 [8, 4096], P(None, 'chan'), may hold values from -6 to 6
- drive_gate: bfloat16 [2048, 8, 4096], P('tm', None, 'chan'), may hold values from -16 to 4
- drive_candidate: bfloat16 [2048, 8, 4096], P('tm', None, 'chan'), may hold values from -6 to 6
- gate_weight: bfloat16 [4096, 4096], P('chan'), may hold values from -0.0234375 to 0.0234375
- candidate_weight: bfloat16 [4096, 4096], P('chan'), may hold values from -0.09375 to 0.09375
Outputs:
- newton_states: float32 [2048, 8, 4096], P('tm', None, 'chan')
- residual_norm: float32 [], replicated
All inputs are finite; a program needn't handle non-finite values.
Results may differ from a plain program's by a relative error of at most 0.0016.
Values may be sent and summed in bfloat16 or wider, within the bound.
A program may use at most 128 MiB of HBM per device.

v0:
```python
import jax
import jax.numpy as jnp
from jax import lax
from jax.sharding import Mesh
from jax.sharding import PartitionSpec as P

TM = ("tm_0", "tm_1", "tm_2")
CHAN_TM = ("chan", "tm_0", "tm_1", "tm_2")


def passed_along(shard, axis, by):
    size = lax.axis_size(axis)
    pairs = [(i, i + by) for i in range(size) if 0 <= i + by < size]
    return lax.ppermute(shard, axis, pairs)


def copy_for_each(shard, axis):
    size = lax.axis_size(axis)
    return lax.all_to_all(
        jnp.broadcast_to(shard[None], (size, *shard.shape)), axis, 0, 0, tiled=True
    )


def collected_together(shard, axis):
    leaves = jax.tree.leaves(shard)
    sequence = sorted(range(len(leaves)), key=lambda k: -leaves[k].size)
    width = (1, *leaves[sequence[0]].shape)[-1]
    lines = [
        jnp.pad(leaves[k].reshape(-1), (0, -leaves[k].size % width)).reshape(-1, width)
        for k in sequence
    ]
    both, at, found = (copy_for_each(jnp.concatenate(lines), axis), 0, {})
    for k, line in zip(sequence, lines):
        piece = both[:, at : at + len(line)].reshape(len(both), -1)
        found[k] = piece[:, : leaves[k].size].reshape(-1, *leaves[k].shape)
        at += len(line)
    numbers = iter(range(len(leaves)))
    return jax.tree.map(lambda _: found[next(numbers)], shard)


def joined_by_halves(pieces, combine):
    while len(jax.tree.leaves(pieces)[0]) > 1:
        pieces = jax.vmap(combine)(
            *(jax.tree.map(lambda part: part[side::2], pieces) for side in (0, 1))
        )
    return jax.tree.map(lambda part: part[0], pieces)


def carried_in(shard, axis, combine, identity):
    size, index = (lax.axis_size(axis), lax.axis_index(axis))
    passed = jnp.arange(size) < index

    def kept(part, zero, own):
        part = jnp.where(
            passed.reshape(-1, *(1 for _ in own.shape)), part, jnp.asarray(zero, own.dtype)
        )
        return part

    pieces = collected_together(shard, axis)
    return joined_by_halves(jax.tree.map(kept, pieces, identity, shard), combine)


def over_axes(shard, axes):
    for axis in axes:
        shard = lax.psum(shard, axis)
    return shard


def combine_maps(earlier, later):
    return (later[0] * earlier[0], later[0] * earlier[1] + later[1])


def local(trajectory, initial, drive_gate, drive_candidate, gate_weight, candidate_weight):
    local_width = trajectory.shape[2]
    chan_index = lax.axis_index("chan")
    time_index = lax.axis_index(TM)
    final_row = trajectory[-1]
    arrived = passed_along(final_row, TM, 1)
    before = jnp.where(time_index == 0, initial, arrived)
    previous = jnp.concatenate([before[None], trajectory[:-1]], 0)
    flat_rows = previous.reshape(-1, local_width).astype(jnp.bfloat16)
    gate_columns, cand_columns = (
        lax.all_to_all(gate_weight, "chan", split_axis=1, concat_axis=0, tiled=True),
        lax.all_to_all(candidate_weight, "chan", split_axis=1, concat_axis=0, tiled=True),
    )
    section = lax.all_gather(flat_rows, "chan", axis=1, tiled=True)
    gate_sum = jnp.dot(section, gate_columns, preferred_element_type=jnp.float32)
    cand_sum = jnp.dot(section, cand_columns, preferred_element_type=jnp.float32)
    gate_block = lax.dynamic_slice_in_dim(gate_columns, chan_index * local_width, local_width, 0)
    cand_block = lax.dynamic_slice_in_dim(cand_columns, chan_index * local_width, local_width, 0)
    gate_diagonal = jnp.diagonal(gate_block).astype(jnp.float32)
    cand_diagonal = jnp.diagonal(cand_block).astype(jnp.float32)
    gate_pre = gate_sum.reshape(previous.shape) + drive_gate.astype(jnp.float32)
    cand_pre = cand_sum.reshape(previous.shape) + drive_candidate.astype(jnp.float32)
    update = jax.nn.sigmoid(gate_pre)
    candidate = jnp.tanh(cand_pre)
    mapped = (1.0 - update) * previous + update * candidate
    jacobian = (
        1.0
        - update
        + update * (1.0 - update) * (candidate - previous) * gate_diagonal
        + update * (1.0 - candidate * candidate) * cand_diagonal
    )
    offset = mapped - jacobian * previous
    ones_state = jnp.ones_like(initial)
    zeros_state = jnp.zeros_like(initial)
    running_product, running_state = lax.associative_scan(combine_maps, (jacobian, offset), axis=0)
    block_product = running_product[-1]
    block_state = running_state[-1]
    prefix_product, prefix_state = carried_in(
        (block_product, block_state), TM, combine_maps, (ones_state, zeros_state)
    )
    entry_state = prefix_product * initial + prefix_state
    newton_states = running_product * entry_state[None] + running_state
    missing = trajectory - mapped
    squared_total = over_axes(jnp.sum(missing * missing), CHAN_TM)
    entries = trajectory.size * lax.axis_size("chan") * lax.axis_size(TM)
    residual_norm = jnp.sqrt(squared_total / entries + 1e-06)
    return (newton_states, residual_norm)


def solution(mesh):
    torus = Mesh(
        mesh.devices.reshape(mesh.shape["chan"], 4, 4, 2), ("chan", "tm_0", "tm_1", "tm_2")
    )
    placed = (
        P(TM, None, "chan"),
        P(None, "chan"),
        P(TM, None, "chan"),
        P(TM, None, "chan"),
        P("chan", None),
        P("chan", None),
    )
    return jax.shard_map(
        local, mesh=torus, in_specs=placed, out_specs=(P(TM, None, "chan"), P()), check_vma=False
    )
```

profile of v0, /device:TPU:1, one launch (start us, length us, event | category | flops | bytes accessed | tf_op | source)
XLA Modules:
  0.0 399.9 jit_solution(14688667386436741681)
XLA Ops:
  7.2 4.6 %copy.17 = bf16[64,8,8,512]{3,2,0,1:T(8,128)(2,1)} copy(bf16[64,8,8,512]{3,2,1,0:T(8,128)(2,1)} %bitcast.66) | data formatting | bytes 8388608 | tf_op jit(solution)/shard_map/all_to_all | solution.py:83
  11.7 9.1 %all-to-all-start = ((bf16[512,8,512]{2,0,1:T(8,128)(2,1)}), bf16[512,8,512]{2,0,1:T(8,128)(2,1)}, u32[]{:S(2)}, u32[]{:S(2)}) async-start(bf16[512,8,512]{2,0,1:T(8,128)(2,1)} %bitcast.65), calls=%async_computation | async-start | bytes 8388608 | tf_op jit(solution)/shard_map/all_to_all | solution.py:83
  20.9 4.0 %collective-permute-start = (f32[8,512]{1,0:T(8,128)S(1)}, f32[8,512]{1,0:T(8,128)S(1)}, u32[]{:S(2)}, u32[]{:S(2)}) collective-permute-start(f32[8,512]{1,0:T(8,128)S(1)} %slice_bitcast_fusion), channel_id=1, source_target_pairs={{0,1},{1,2},{2,3},{3,4},{4,5},{5,6},{6,7},{7,8},{8,9},{9,10},{10,1... | collective-permute-start | bytes 49160 | tf_op jit(solution)/shard_map/ppermute | solution.py:14
  25.0 4.6 %copy.16 = bf16[64,8,8,512]{3,2,0,1:T(8,128)(2,1)} copy(bf16[64,8,8,512]{3,2,1,0:T(8,128)(2,1)} %bitcast.67) | data formatting | bytes 8388608 | tf_op jit(solution)/shard_map/all_to_all | solution.py:84
  29.6 88.1 %all-to-all-done = bf16[512,8,512]{2,0,1:T(8,128)(2,1)} async-done(((bf16[512,8,512]{2,0,1:T(8,128)(2,1)}), bf16[512,8,512]{2,0,1:T(8,128)(2,1)}, u32[]{:S(2)}, u32[]{:S(2)}) %all-to-all-start) | async-done | bytes 4194336 | tf_op jit(solution)/shard_map/all_to_all | solution.py:83
  117.7 4.7 %all-to-all-start.1 = ((bf16[512,8,512]{2,0,1:T(8,128)(2,1)}), bf16[512,8,512]{2,0,1:T(8,128)(2,1)}, u32[]{:S(2)}, u32[]{:S(2)}) async-start(bf16[512,8,512]{2,0,1:T(8,128)(2,1)} %bitcast.64), calls=%async_computation.1 | async-start | bytes 8388608 | tf_op jit(solution)/shard_map/all_to_all | solution.py:84
  122.6 0.9 convert_bitcast_fusion
  123.5 132.7 %all-to-all-done.1 = bf16[512,8,512]{2,0,1:T(8,128)(2,1)} async-done(((bf16[512,8,512]{2,0,1:T(8,128)(2,1)}), bf16[512,8,512]{2,0,1:T(8,128)(2,1)}, u32[]{:S(2)}, u32[]{:S(2)}) %all-to-all-start.1) | async-done | bytes 4194336 | tf_op jit(solution)/shard_map/all_to_all | solution.py:84
  256.1 1.3 constant_dynamic-slice_fusion
  257.4 4.8 %gather_fusion = bf16[512]{0:T(512)(128)(2,1)S(1)} fusion(bf16[512,512]{1,0:T(8,128)(2,1)S(1)} %get-tuple-element.42, s32[512]{0:T(512)S(1)} %bitcast.62), kind=kCustom, calls=%fused_computation | custom fusion | bytes 6144 | tf_op jit(solution)/shard_map/jit(diagonal)/cond/branch_0_fun/gather | solution.py:91
  262.3 4.8 %gather_fusion.1 = bf16[512]{0:T(512)(128)(2,1)S(1)} fusion(bf16[512,512]{1,0:T(8,128)(2,1)S(1)} %get-tuple-element.41, s32[512]{0:T(512)S(1)} %bitcast.63), kind=kCustom, calls=%fused_computation.1 | custom fusion | bytes 6144 | tf_op jit(solution)/shard_map/jit(diagonal)/cond/branch_0_fun/gather | solution.py:92
  267.2 5.9 %fusion.22 = f32[64,8,512]{2,1,0:T(8,128)S(1)} fusion(bf16[4096,512,1]{1,0,2:T(8,128)(2,1)} %bitcast.9, bf16[512,4096]{1,0:T(8,128)(2,1)} %all-gather.2.cloned.1.call-done, bf16[64,8,512]{2,1,0:T(8,128)(2,1)S(1)} %copy-done.8), kind=kOutput, calls=%fused_computation.17 | convolution fusion | flops 2148007936 | bytes 9961472 | tf_op jit(solution)/shard_map/dot_general | solution.py:88
  273.2 6.0 %fusion.27 = (f32[64,8,512]{2,1,0:T(8,128)S(1)}, f32[64,8,512]{2,1,0:T(8,128)S(1)}, f32[]{:T(128)}) fusion(f32[64,8,512]{2,1,0:T(8,128)S(1)} %fusion.22, f32[512]{0:T(512)S(1)} %convert_element_type.31, f32[512]{0:T(512)S(1)} %convert_element_type.30, f32[63,8,512]{2,1,0:T(8,128)S(1)} %slice.253, f32[1,8,512]{2,1,0:T(8,128)S(1)} %select_bitcast_fusion, ...), kind=kOutput, calls=%fused_computation.20 | convolution fusion | flops 2154037248 | bytes 14159876 | tf_op jit(solution)/shard_map/dot_general | solution.py:87
  279.2 1.0 copy-done.1
  284.9 1.0 pad_maximum_fusion.4
  286.0 5.8 %pad.95 = f32[32,8,512]{2,1,0:T(8,128)S(1)} pad(f32[16,8,512]{2,1,0:T(8,128)} %add.212, f32[]{:T(128)} %constant.41.clone.1), padding=1_0_1x0_0_0x0_0_0 | pad | bytes 786436 | tf_op jit(solution)/shard_map/pad | solution.py:107
  291.8 0.9 add.197
  292.7 2.3 add_multiply_fusion.1
  295.0 0.9 add.214
  295.9 11.6 %pad.85 = f32[64,8,512]{2,1,0:T(8,128)S(1)} pad(f32[32,8,512]{2,1,0:T(8,128)} %add.197, f32[]{:T(128)} %constant.41.clone.1), padding=1_0_1x0_0_0x0_0_0 | pad | bytes 1572868 | tf_op jit(solution)/shard_map/pad | solution.py:107
  307.5 1.1 pad_maximum_fusion.1
  308.8 11.6 %pad.97 = f32[64,8,512]{2,1,0:T(8,128)S(1)} pad(f32[32,8,512]{2,1,0:T(8,128)} %add.214, f32[]{:T(128)} %constant.41.clone.1), padding=1_0_1x0_0_0x0_0_0 | pad | bytes 1572868 | tf_op jit(solution)/shard_map/pad | solution.py:107
  320.4 1.9 pad_maximum_fusion.2
  322.3 15.6 %pad.96 = f32[64,8,512]{2,1,0:T(8,128)} pad(f32[32,8,512]{2,1,0:T(8,128)} %pad_maximum_fusion.2, f32[]{:T(128)} %constant.41.clone.1), padding=0_1_1x0_0_0x0_0_0 | pad | bytes 1572868 | tf_op jit(solution)/shard_map/pad | solution.py:107
  338.7 1.1 broadcast_in_dim.40
  339.8 8.1 %all-to-all-start.2 = ((f32[32,16,512]{2,1,0:T(8,128)}), f32[32,16,512]{2,1,0:T(8,128)}, u32[]{:S(2)}, u32[]{:S(2)}) async-start(f32[32,16,512]{2,1,0:T(8,128)} %broadcast_in_dim.40), calls=%async_computation.2 | async-start | bytes 2097152 | tf_op jit(solution)/shard_map/all_to_all | solution.py:19
  347.9 12.6 %psum.28 = f32[]{:T(128)} all-reduce(f32[]{:T(128)} %get-tuple-element.4), channel_id=1, replica_groups=mesh['chan'=8,'tm_0'=4,'tm_1'=4,'tm_2'=2] {'chan'}, use_global_device_ids=true, to_apply=%region_1.2 | all-reduce | flops 1 | bytes 8 | tf_op jit(solution)/shard_map/psum | solution.py:65
  360.5 9.4 %psum.29 = f32[]{:T(128)} all-reduce(f32[]{:T(128)} %psum.28), channel_id=1, replica_groups=mesh['chan'=8,'tm_0'=4,'tm_1'=4,'tm_2'=2] {'tm_0'}, use_global_device_ids=true, to_apply=%region_2.3 | all-reduce | flops 1 | bytes 8 | tf_op jit(solution)/shard_map/psum | solution.py:65
  369.9 9.0 %psum.30 = f32[]{:T(128)} all-reduce(f32[]{:T(128)} %psum.29), channel_id=1, replica_groups=mesh['chan'=8,'tm_0'=4,'tm_1'=4,'tm_2'=2] {'tm_1'}, use_global_device_ids=true, to_apply=%region_3.4 | all-reduce | flops 1 | bytes 8 | tf_op jit(solution)/shard_map/psum | solution.py:65
  378.9 9.2 %psum.31 = f32[]{:T(128)} all-reduce(f32[]{:T(128)} %psum.30), channel_id=1, replica_groups=mesh['chan'=8,'tm_0'=4,'tm_1'=4,'tm_2'=2] {'tm_2'}, use_global_device_ids=true, to_apply=%region_4.5 | all-reduce | flops 1 | bytes 8 | tf_op jit(solution)/shard_map/psum | solution.py:65
  388.8 1.4 slice_select_fusion.1
  390.4 1.5 multiply_add_fusion
  (88 shorter events, 6.0 us)
Async XLA Ops:
  11.7 9.1 %copy-start.2 = (f32[64,8,512]{2,1,0:T(8,128)S(1)}, f32[64,8,512]{2,1,0:T(8,128)}, u32[]{:S(2)}) copy-start(f32[64,8,512]{2,1,0:T(8,128)} %param.6) | copy-start | bytes 3145732
  11.7 106.0 %all-to-all-start = ((bf16[512,8,512]{2,0,1:T(8,128)(2,1)}), bf16[512,8,512]{2,0,1:T(8,128)(2,1)}, u32[]{:S(2)}, u32[]{:S(2)}) async-start(bf16[512,8,512]{2,0,1:T(8,128)(2,1)} %bitcast.65), calls=%async_computation | async-start | bytes 8388608 | tf_op jit(solution)/shard_map/all_to_all | solution.py:83
  20.9 101.6 %collective-permute-start = (f32[8,512]{1,0:T(8,128)S(1)}, f32[8,512]{1,0:T(8,128)S(1)}, u32[]{:S(2)}, u32[]{:S(2)}) collective-permute-start(f32[8,512]{1,0:T(8,128)S(1)} %slice_bitcast_fusion), channel_id=1, source_target_pairs={{0,1},{1,2},{2,3},{3,4},{4,5},{5,6},{6,7},{7,8},{8,9},{9,10},{10,1... | collective-permute-start | bytes 49160 | tf_op jit(solution)/shard_map/ppermute | solution.py:14
  117.7 4.8 %copy-start.5 = (f32[8,512]{1,0:T(8,128)S(1)}, f32[8,512]{1,0:T(8,128)}, u32[]{:S(2)}) copy-start(f32[8,512]{1,0:T(8,128)} %param.7) | copy-start | bytes 49156
  117.7 138.4 %all-to-all-start.1 = ((bf16[512,8,512]{2,0,1:T(8,128)(2,1)}), bf16[512,8,512]{2,0,1:T(8,128)(2,1)}, u32[]{:S(2)}, u32[]{:S(2)}) async-start(bf16[512,8,512]{2,0,1:T(8,128)(2,1)} %bitcast.64), calls=%async_computation.1 | async-start | bytes 8388608 | tf_op jit(solution)/shard_map/all_to_all | solution.py:84
  122.5 144.7 %copy-start.8 = (bf16[64,8,512]{2,1,0:T(8,128)(2,1)S(1)}, bf16[64,8,512]{2,1,0:T(8,128)(2,1)}, u32[]{:S(2)}) copy-start(bf16[64,8,512]{2,1,0:T(8,128)(2,1)} %param.9) | copy-start | bytes 1572868
  122.5 144.7 %all-gather.2.cloned.1.call-start = ((), (), s32[]{:S(2)}) async-start(), calls=%async_computation.3 | async-start | bytes 4718592 | tf_op jit(solution)/shard_map/all_gather | solution.py:86
  267.2 6.0 %copy-start.3 = (f32[64,8,512]{2,1,0:T(8,128)S(1)}, f32[64,8,512]{2,1,0:T(8,128)}, u32[]{:S(2)}) copy-start(f32[64,8,512]{2,1,0:T(8,128)} %param.6) | copy-start | bytes 3145732
  267.2 6.0 %copy-start.7 = (bf16[512,4096]{1,0:T(8,128)(2,1)S(1)}, bf16[512,4096]{1,0:T(8,128)(2,1)}, u32[]{:S(2)}) copy-start(bf16[512,4096]{1,0:T(8,128)(2,1)} %all-gather.2.cloned.1.call-done) | copy-start | bytes 12582916
  267.2 6.0 %copy-start.9 = (bf16[64,8,512]{2,1,0:T(8,128)(2,1)S(1)}, bf16[64,8,512]{2,1,0:T(8,128)(2,1)}, u32[]{:S(2)}) copy-start(bf16[64,8,512]{2,1,0:T(8,128)(2,1)} %param.8) | copy-start | bytes 1572868
  279.2 1.0 copy-start.1
  281.8 2.7 copy-start.4
  337.9 52.5 %copy-start.6 = (f32[8,512]{1,0:T(8,128)S(1)}, f32[8,512]{1,0:T(8,128)}, u32[]{:S(2)}) copy-start(f32[8,512]{1,0:T(8,128)} %param.7) | copy-start | bytes 49156
  339.8 49.0 %all-to-all-start.2 = ((f32[32,16,512]{2,1,0:T(8,128)}), f32[32,16,512]{2,1,0:T(8,128)}, u32[]{:S(2)}, u32[]{:S(2)}) async-start(f32[32,16,512]{2,1,0:T(8,128)} %broadcast_in_dim.40), calls=%async_computation.2 | async-start | bytes 2097152 | tf_op jit(solution)/shard_map/all_to_all | solution.py:19
  388.8 1.7 copy-start
Sparse Core Ops, SparseCore 0:
  125.7 129.5 all-gather.1
where the time goes:
time: 404 us; the launch traced here: 400 us
  waiting for transfers between devices  221 us (55%)
  local copies, waits for them, and re-layouts  69.5 us (17%)
  blocking collectives  40.2 us (10%)
  starting transfers between devices  26 us (6%)
  between operations  16.5 us (4%)
  other arithmetic  14.9 us (4%)
  matrix products  11.9 us (3%)
    all_to_all x1, waiting for transfers between devices, local(): lax.all_to_all(candidate_weight, 'chan', split_axis=1, concat_axis=0, til...  133 us
    all_to_all x1, waiting for transfers between devices, local(): lax.all_to_all(gate_weight, 'chan', split_axis=1, concat_axis=0, tiled=True)  88.1 us
    pad x20, local copies, waits for them, and re-layouts, local(): lax.associative_scan(combine_maps, (jacobian, offset), axis=0)  45.9 us
    psum x4, blocking collectives, over_axes(): shard = lax.psum(shard, axis)  40.2 us
    all_to_all x1, starting transfers between devices, local(): lax.all_to_all(gate_weight, 'chan', split_axis=1, concat_axis=0, tiled=True)  9.13 us
  transfers between devices with their start and end apart: 5, of which 2 were waited for; matrix products, arithmetic and copies ran while one was open for 4% of the time, Pallas kernels for 0%

commit v1 on v0

v1 whole, which is shorter than its diff:
```python
import jax
import jax.numpy as jnp
from jax import lax
from jax.experimental import pallas as pl
from jax.experimental.pallas import tpu as pltpu
from jax.sharding import Mesh
from jax.sharding import PartitionSpec as P

MESH = pl.DeviceIdType.MESH
AXES = ("chan", "tm_x", "tm_y", "tm_c")
TM = AXES[1:]
NZ, NX, NY, NC = 8, 4, 4, 2
STEPS, BATCH, WIDTH = 64, 8, 512
ROWS = STEPS * BATCH
PIECES = 4
PIECE = ROWS // PIECES
PIECE_STEPS = STEPS // PIECES
SHARES = 16
SHARE = WIDTH // SHARES
ENTRIES = 2048 * 8 * 4096
ORDER = (1, 2, 3, 0)
LAST = ((ORDER[0], ORDER[2]), (ORDER[1], ORDER[3]))
TILES = WIDTH // 128


def arrivals(way):
    return [(d, q) for d in (1, 2, 3) for q in ORDER] + [(4, q) for q in LAST[way]]


def kernel(
    traj, init, dgate, dcand, gate_w, cand_w, out, res,
    A, W, acc, trv, dgv, dcv, first_in, first, maps, sib_map, y_maps, x_maps, z_sums,
    local_sem, bound_s, bound_r, a_s, a_r, wz_s, wz_r, p1_s, p1_r, p1b_s, p1b_r,
    p2_s, p2_r, p2b_s, p2b_r, d_s, d_r, m_s, m_r,
):
    z, x, y, c = (lax.axis_index(a) for a in AXES)
    t = (x * NY + y) * NC + c

    def at_time(k):
        k = lax.rem(k + NX * NY * NC, NX * NY * NC)
        return (z, k // (NY * NC), lax.rem(k // NC, NY), lax.rem(k, NC))

    def at_z(d):
        return (lax.rem(z + d + NZ, NZ), x, y, c)

    def at_x(d):
        return (z, lax.rem(x + d + NX, NX), y, c)

    def at_y(d):
        return (z, x, lax.rem(y + d + NY, NY), c)

    sibling = (z, x, y, 1 - c)
    me1 = x * (1 - c) + y * c
    me2 = y * (1 - c) + x * c

    def ring1(d):
        return (z, lax.rem(x + d * (1 - c) + NX, NX), lax.rem(y + d * c + NY, NY), c)

    def ring2(d):
        return (z, lax.rem(x + d * c + NX, NX), lax.rem(y + d * (1 - c) + NY, NY), c)

    def share(d2, d1):
        return lax.rem(me2 + d2 + 4, 4) * 4 + lax.rem(me1 + d1 + 4, 4)

    def remote(src, dst, s, r, to):
        return pltpu.make_async_remote_copy(
            src_ref=src, dst_ref=dst, send_sem=s, recv_sem=r, device_id=to, device_id_type=MESH
        )

    loads = [
        pltpu.make_async_copy(src, dst, local_sem.at[k])
        for k, (src, dst) in enumerate(
            ((traj, trv), (dgate, dgv), (dcand, dcv), (init, first_in.at[0]))
        )
    ]
    loads[0].start()

    barrier = pltpu.get_barrier_semaphore()
    peers = (
        [at_z(d) for d in range(1, NZ)]
        + [at_x(d) for d in range(1, NX)]
        + [at_y(d) for d in range(1, NY)]
        + [sibling, at_time(t + 1), at_time(t - 1)]
    )
    for peer in peers:
        pl.semaphore_signal(barrier, inc=1, device_id=peer, device_id_type=MESH)
    mine = share(0, 0)
    own_rows = pl.ds(pl.multiple_of(mine * SHARE, SHARE), SHARE)

    def columns(k):
        return pl.ds(pl.multiple_of(k * WIDTH, WIDTH), WIDTH)

    own_block = W.at[c, mine, z]

    @pl.when(c == 0)
    def _():
        pltpu.make_async_copy(gate_w.at[own_rows, columns(z)], own_block, local_sem.at[4]).start()

    @pl.when(c == 1)
    def _():
        pltpu.make_async_copy(cand_w.at[own_rows, columns(z)], own_block, local_sem.at[4]).start()

    for load in loads[1:]:
        load.start()
    loads[0].wait()
    for q in range(1, PIECES):
        A[z, q] = (
            trv[q * PIECE_STEPS - 1 : (q + 1) * PIECE_STEPS - 1]
            .reshape(PIECE, WIDTH)
            .astype(jnp.bfloat16)
        )
    pl.semaphore_wait(barrier, len(peers))

    boundary = remote(trv.at[STEPS - 1], first_in.at[1], bound_s, bound_r, at_time(t + 1))
    boundary.start()

    def spread(ref):
        for d in range(1, NZ):
            to = at_z(d)
            remote(ref.at[own_rows, columns(to[0])], W.at[c, mine, z], wz_s, wz_r, to).start()

    @pl.when(c == 0)
    def _():
        spread(gate_w)

    @pl.when(c == 1)
    def _():
        spread(cand_w)

    def a_copy(way, i):
        d, q = arrivals(way)[i]
        sign = 1 - 2 * way
        block = A.at[lax.rem(z - sign * (d - 1) + NZ, NZ), q]
        return remote(block, block, a_s.at[way, i], a_r.at[way, i], at_z(sign))

    def a_arrived(way, i):
        d, q = arrivals(way)[i]
        sign = 1 - 2 * way
        block = A.at[lax.rem(z - sign * d + NZ, NZ), q]
        remote(block, block, a_s.at[way, i], a_r.at[way, i], at_z(sign)).wait_recv()

    def a_event(i):
        for way in (0, 1):
            a_arrived(way, i)
            d, q = arrivals(way)[i]
            if (d + 1, q) in arrivals(way):
                a_copy(way, arrivals(way).index((d + 1, q))).start()

    for i in range(3):
        for way in (0, 1):
            a_copy(way, i).start()
    boundary.wait_recv()
    loads[3].wait()
    first[...] = jnp.where(t == 0, first_in[0], first_in[1])
    A[z, 0] = (
        jnp.concatenate([first[...][None], trv[: PIECE_STEPS - 1]], 0)
        .reshape(PIECE, WIDTH)
        .astype(jnp.bfloat16)
    )

    def whole(d2, d1):
        return W.at[c, share(d2, d1)]

    def to_sibling(d2, d1):
        block = whole(d2, d1)
        return remote(block, block, d_s, d_r, sibling)

    def p1(way):
        block = whole(0, 0)
        return remote(block, block, p1_s.at[way], p1_r.at[way], ring1(1 - 2 * way))

    def p1_arrived(way):
        block = whole(0, 2 * way - 1)
        remote(block, block, p1_s.at[way], p1_r.at[way], ring1(1 - 2 * way)).wait_recv()

    def p1b(way):
        block = W.at[c, share(0, 2 * way - 1), pl.ds(way * 4, 4)]
        return remote(block, block, p1b_s.at[way], p1b_r.at[way], ring1(1 - 2 * way))

    def p1b_arrived(way):
        block = W.at[c, share(0, 2), pl.ds(way * 4, 4)]
        remote(block, block, p1b_s.at[way], p1b_r.at[way], ring1(1 - 2 * way)).wait_recv()

    along = (0, -1, 1, 2)

    def p2(way, j):
        block = whole(0, along[j])
        return remote(block, block, p2_s.at[way, j], p2_r.at[way, j], ring2(1 - 2 * way))

    def p2_arrived(way, j):
        block = whole(2 * way - 1, along[j])
        remote(block, block, p2_s.at[way, j], p2_r.at[way, j], ring2(1 - 2 * way)).wait_recv()

    def p2b(j):
        way = j % 2
        block = whole(2 * way - 1, along[j])
        return remote(block, block, p2b_s.at[j], p2b_r.at[j], ring2(1 - 2 * way))

    def p2b_arrived(j):
        block = whole(2, along[j])
        remote(block, block, p2b_s.at[j], p2b_r.at[j], ring2(1 - 2 * (j % 2))).wait_recv()

    def p2_event(j):
        for way in (0, 1):
            p2_arrived(way, j)
            if j % 2 == way:
                p2b(j).start()
            to_sibling(2 * way - 1, along[j]).start()

    def start_share(j):
        p2(0, j).start()
        p2(1, j).start()
        to_sibling(0, along[j]).start()

    seven = W.at[c, mine, pl.ds(0, NZ - 1)]
    pltpu.make_async_copy(own_block, own_block, local_sem.at[4]).wait()
    remote(seven, seven, wz_s, wz_r, at_z(1)).wait_recv()
    p1(0).start()
    p1(1).start()
    start_share(0)
    for way in (0, 1):
        a_copy(way, 3).start()
    a_event(0)
    a_event(1)
    for way in (0, 1):
        p1_arrived(way)
        p1b(way).start()
        start_share(1 + way)
    a_event(2)
    p2_event(0)
    for way in (0, 1):
        p1b_arrived(way)
    start_share(3)
    a_event(3)
    a_event(4)
    p2_event(1)
    p2_event(2)
    a_event(5)
    a_event(6)
    p2_event(3)
    a_event(7)
    for j in range(4):
        p2b_arrived(j)
        to_sibling(2, along[j]).start()
    theirs = W.at[1 - c]
    a_event(8)
    remote(theirs, theirs, d_s, d_r, sibling).wait_recv()

    def half(n):
        return pl.ds(pl.multiple_of(n * 256, 256), 256)

    def product(k, m, n):
        return jnp.dot(
            A[k].reshape(ROWS, WIDTH),
            W[m, :, k, :, half(n)].reshape(WIDTH, 256),
            preferred_element_type=jnp.float32,
        )

    def at(d):
        return lax.rem(z + d + NZ, NZ)

    def gather_sums(ds, fresh):
        def body(i, carry):
            m, n = i // 2, lax.rem(i, 2)
            total = product(at(ds[0]), m, n)
            for d in ds[1:]:
                total = total + product(at(d), m, n)
            if not fresh:
                total = total + acc[m, :, half(n)]
            acc[m, :, half(n)] = total
            return carry

        lax.fori_loop(0, 4, body, 0)

    gather_sums((0, 1, -1), True)
    a_event(9)
    gather_sums((2, -2), False)
    a_event(10)
    eye = lax.broadcasted_iota(jnp.int32, (WIDTH, WIDTH), 0) == lax.broadcasted_iota(
        jnp.int32, (WIDTH, WIDTH), 1
    )

    def diagonal(m):
        block = W[m, :, z].reshape(WIDTH, WIDTH).astype(jnp.float32)
        return jnp.sum(jnp.where(eye, block, 0.0), axis=0, keepdims=True)

    gate_diag = diagonal(0)
    cand_diag = diagonal(1)
    loads[1].wait()
    loads[2].wait()
    a_event(11)
    gather_sums((3, -3), False)

    far = at(4)
    ones = jnp.ones((BATCH, WIDTH), jnp.float32)
    zeros = jnp.zeros((BATCH, WIDTH), jnp.float32)

    def finish(q, squares):
        rows = pl.ds(q * PIECE, PIECE)
        for m in (0, 1):
            acc[m, rows, :] += jnp.dot(
                A[far, q], W[m, :, far].reshape(WIDTH, WIDTH), preferred_element_type=jnp.float32
            )
        group = 4

        def body(i, carry):
            prod, state, squares = carry
            s0 = q * PIECE_STEPS + i * group
            here = pl.ds(pl.multiple_of(s0 * BATCH, group * BATCH), group * BATCH)
            steps = pl.ds(s0, group)
            now = trv[steps]
            if q == 0:
                before = jnp.where(i == 0, first[...], trv[jnp.maximum(s0 - 1, 0)])
            else:
                before = trv[s0 - 1]
            prev = jnp.concatenate([before[None], now[: group - 1]], 0)
            shape = (group, BATCH, WIDTH)
            update = jax.nn.sigmoid(
                acc[0, here, :].reshape(shape) + dgv[steps].astype(jnp.float32)
            )
            cand = jnp.tanh(acc[1, here, :].reshape(shape) + dcv[steps].astype(jnp.float32))
            keep = 1.0 - update
            mapped = keep * prev + update * cand
            jac = (
                keep
                + update * keep * (cand - prev) * gate_diag[None]
                + update * (1.0 - cand * cand) * cand_diag[None]
            )
            offset = mapped - jac * prev
            missing = now - mapped
            squares = squares + jnp.sum(missing * missing, axis=0)
            acc[0, here, :] = jac.reshape(group * BATCH, WIDTH)
            acc[1, here, :] = offset.reshape(group * BATCH, WIDTH)
            for k in range(group):
                prod = jac[k] * prod
                state = jac[k] * state + offset[k]
            return prod, state, squares

        return lax.fori_loop(0, PIECE_STEPS // group, body, (ones, zeros, squares))

    squares = zeros
    found = {}
    for i in (12, 13):
        a_event(i)
        for way in (0, 1):
            q = arrivals(way)[i][1]
            prod, state, squares = finish(q, squares)
            found[q] = (prod, state)

    prod, state = found[0]
    for q in range(1, PIECES):
        prod, state = found[q][0] * prod, found[q][0] * state + found[q][1]

    def store_map(ref, prod, state, square):
        for k in range(TILES):
            ref[k] = prod[:, k * 128 : (k + 1) * 128]
            ref[TILES + k] = state[:, k * 128 : (k + 1) * 128]
        ref[2 * TILES] = square

    def load_map(ref):
        return (
            jnp.concatenate([ref[k] for k in range(TILES)], axis=1),
            jnp.concatenate([ref[TILES + k] for k in range(TILES)], axis=1),
            ref[2 * TILES],
        )

    square = squares[:, :128]
    for k in range(1, TILES):
        square = square + squares[:, k * 128 : (k + 1) * 128]
    store_map(maps.at[0], prod, state, square)
    sib = remote(maps.at[0], sib_map, m_s.at[0], m_r.at[0], sibling)
    sib.start()
    sib.wait_recv()
    s_prod, s_state, s_square = load_map(sib_map)
    odd = c == 1
    e_prod, e_state = jnp.where(odd, s_prod, prod), jnp.where(odd, s_state, state)
    l_prod, l_state = jnp.where(odd, prod, s_prod), jnp.where(odd, state, s_state)
    store_map(maps.at[1], l_prod * e_prod, l_prod * e_state + l_state, square + s_square)

    def exchange(k, slots, count, index, peer):
        for d in range(1, count):
            remote(maps.at[k], slots.at[index], m_s.at[k], m_r.at[k], peer(d)).start()
        slots[index] = maps[k]
        three = slots.at[pl.ds(0, count - 1)]
        remote(three, three, m_s.at[k], m_r.at[k], peer(1)).wait_recv()

    exchange(1, y_maps, NY, y, at_y)
    total = load_map(y_maps.at[0])
    for k in range(1, NY):
        n_prod, n_state, n_square = load_map(y_maps.at[k])
        total = (n_prod * total[0], n_prod * total[1] + n_state, total[2] + n_square)
    store_map(maps.at[2], *total)
    exchange(2, x_maps, NX, x, at_x)

    square = x_maps[0, 2 * TILES]
    for k in range(1, NX):
        square = square + x_maps[k, 2 * TILES]
    maps[3, 0] = square
    for d in range(1, NZ):
        remote(maps.at[3, 0], z_sums.at[z], m_s.at[3], m_r.at[3], at_z(d)).start()

    value = first_in[0]
    for k in range(NX - 1):
        n_prod, n_state, _ = load_map(x_maps.at[k])
        value = jnp.where(k < x, n_prod * value + n_state, value)
    for k in range(NY - 1):
        n_prod, n_state, _ = load_map(y_maps.at[k])
        value = jnp.where(k < y, n_prod * value + n_state, value)
    value = jnp.where(odd, s_prod * value + s_state, value)

    def run(i, value):
        for k in range(4):
            step = i * 4 + k
            here = pl.ds(pl.multiple_of(step * BATCH, BATCH), BATCH)
            value = acc[0, here, :] * value + acc[1, here, :]
            out[step] = value
        return value

    lax.fori_loop(0, STEPS // 4, run, value)

    z_sums[z] = square
    seven_sums = z_sums.at[pl.ds(0, NZ - 1)]
    remote(seven_sums, seven_sums, m_s.at[3], m_r.at[3], at_z(1)).wait_recv()
    square = z_sums[0]
    for k in range(1, NZ):
        square = square + z_sums[k]
    whole_sum = jnp.sum(jnp.sum(square, axis=0, keepdims=True), axis=1, keepdims=True)
    res[...] = jnp.sqrt(whole_sum / ENTRIES + 1e-06)

    boundary.wait_send()
    remote(seven, seven, wz_s, wz_r, at_z(1)).wait_send()
    for way in (0, 1):
        for i in range(len(arrivals(way))):
            a_copy(way, i).wait_send()
        p1(way).wait_send()
        p1b(way).wait_send()
        for j in range(4):
            p2(way, j).wait_send()
    for j in range(4):
        p2b(j).wait_send()
    ours = W.at[c]
    remote(ours, ours, d_s, d_r, sibling).wait_send()
    sib.wait_send()
    for k, slots in ((1, y_maps), (2, x_maps)):
        three = slots.at[pl.ds(0, 3)]
        remote(three, three, m_s.at[k], m_r.at[k], at_y(1)).wait_send()
    remote(seven_sums, seven_sums, m_s.at[3], m_r.at[3], at_z(1)).wait_send()


def local(trajectory, initial, drive_gate, drive_candidate, gate_weight, candidate_weight):
    dma = pltpu.SemaphoreType.DMA
    tiles = (2 * TILES + 1, BATCH, 128)
    states, residual = pl.pallas_call(
        kernel,
        out_shape=(
            jax.ShapeDtypeStruct((STEPS, BATCH, WIDTH), jnp.float32),
            jax.ShapeDtypeStruct((1, 1), jnp.float32),
        ),
        in_specs=[pl.BlockSpec(memory_space=pl.ANY)] * 6,
        out_specs=(
            pl.BlockSpec(memory_space=pltpu.VMEM),
            pl.BlockSpec(memory_space=pltpu.VMEM),
        ),
        scratch_shapes=[
            pltpu.VMEM((NZ, PIECES, PIECE, WIDTH), jnp.bfloat16),
            pltpu.VMEM((2, SHARES, NZ, SHARE, WIDTH), jnp.bfloat16),
            pltpu.VMEM((2, ROWS, WIDTH), jnp.float32),
            pltpu.VMEM((STEPS, BATCH, WIDTH), jnp.float32),
            pltpu.VMEM((STEPS, BATCH, WIDTH), jnp.bfloat16),
            pltpu.VMEM((STEPS, BATCH, WIDTH), jnp.bfloat16),
            pltpu.VMEM((2, BATCH, WIDTH), jnp.float32),
            pltpu.VMEM((BATCH, WIDTH), jnp.float32),
            pltpu.VMEM((4, *tiles), jnp.float32),
            pltpu.VMEM(tiles, jnp.float32),
            pltpu.VMEM((NY, *tiles), jnp.float32),
            pltpu.VMEM((NX, *tiles), jnp.float32),
            pltpu.VMEM((NZ, BATCH, 128), jnp.float32),
            dma((5,)),
            dma,
            dma,
            dma((2, 14)),
            dma((2, 14)),
            dma,
            dma,
            dma((2,)),
            dma((2,)),
            dma((2,)),
            dma((2,)),
            dma((2, 4)),
            dma((2, 4)),
            dma((4,)),
            dma((4,)),
            dma,
            dma,
            dma((4,)),
            dma((4,)),
        ],
        compiler_params=pltpu.CompilerParams(collective_id=0, has_side_effects=True),
    )(trajectory, initial, drive_gate, drive_candidate, gate_weight, candidate_weight)
    return states, residual.reshape(())


def solution(mesh):
    torus = Mesh(mesh.devices.reshape(NZ, NX, NY, NC), AXES)
    placed = (
        P(TM, None, "chan"),
        P(None, "chan"),
        P(TM, None, "chan"),
        P(TM, None, "chan"),
        P("chan", None),
        P("chan", None),
    )
    return jax.shard_map(
        local, mesh=torus, in_specs=placed, out_specs=(P(TM, None, "chan"), P()), check_vma=False
    )
```

time: 404 us -> 78.8 us (0.20)
  waiting for transfers between devices: 221 us -> 0 us
  Pallas kernels: 0 us -> 74.1 us
  local copies, waits for them, and re-layouts: 69.5 us -> 2.26 us
  blocking collectives: 40.2 us -> 0 us
  starting transfers between devices: 26 us -> 0 us
  other arithmetic: 14.9 us -> 0 us
  between operations: 16.5 us -> 2.33 us
  matrix products: 11.9 us -> 0 us
    all_to_all x3 -> x0, waiting for transfers between devices: 221 us -> none  [the longest x1 133 us: local(): lax.all_to_all(candidate_weight, 'chan', split_axis=1, concat_axis=0, til...]
    pallas_call x0 -> x1, Pallas kernels: none -> 74.1 us  [local(): pl.pallas_call(kernel, out_shape=(jax.ShapeDtypeStruct((STEPS, BATCH, WID...]
    pad x20 -> x0, local copies, waits for them, and re-layouts: 45.9 us -> none  [local(): lax.associative_scan(combine_maps, (jacobian, offset), axis=0)]
    psum x4 -> x0, blocking collectives: 40.2 us -> none  [over_axes(): shard = lax.psum(shard, axis)]
    all_to_all x3 -> x0, starting transfers between devices: 21.9 us -> none  [the longest x1 9.13 us: local(): lax.all_to_all(gate_weight, 'chan', split_axis=1, concat_axis=0, tiled=True)]
    dot_general x2 -> x0, matrix products: 11.9 us -> none  [the longest x1 6 us: local(): jnp.dot(section, gate_columns, preferred_element_type=jnp.float32)]
    gather x2 -> x0, local copies, waits for them, and re-layouts: 9.7 us -> none  [the longest x1 4.85 us: local(): gate_diagonal = jnp.diagonal(gate_block).astype(jnp.float32)]
    all_to_all x2 -> x0, local copies, waits for them, and re-layouts: 9.16 us -> none  [the longest x1 4.59 us: local(): lax.all_to_all(candidate_weight, 'chan', split_axis=1, concat_axis=0, til...]
  transfers between devices with their start and end apart: 5 -> 0, of which waited for: 2 -> 0; matrix products, arithmetic and copies ran while one was open for 4% -> 0% of each run, Pallas kernels for 0% -> 0%
where the time goes in v1:
time: 78.8 us; the launch traced here: 78.7 us
  Pallas kernels  74.1 us (94%)
  between operations  2.33 us (3%)
  local copies, waits for them, and re-layouts  2.26 us (3%)
    pallas_call x1, Pallas kernels, local(): pl.pallas_call(kernel, out_shape=(jax.ShapeDtypeStruct((STEPS, BATCH, WID...  74.1 us
    unnamed x1, local copies, waits for them, and re-layouts  2.26 us

profile of v1, /device:TPU:1, one launch (start us, length us, event | category | flops | bytes accessed | tf_op | source)
XLA Modules:
  0.0 78.7 jit_solution(18380367182446692834)
XLA Ops:
  0.6 74.1 %shard_map.77 = (f32[64,8,512]{2,1,0:T(8,128)}, f32[1,1]{1,0:T(1,128)}) custom-call(f32[64,8,512]{2,1,0:T(8,128)} %traj.1, f32[8,512]{1,0:T(8,128)} %init.1, bf16[64,8,512]{2,1,0:T(8,128)(2,1)} %dgate.1, bf16[64,8,512]{2,1,0:T(8,128)(2,1)} %dcand.1, bf16[512,4096]{1,0:T(8,128)(2,1)} %gate_w.1, bf16[512,4096]{1,0:T(8,128)(2,1)} %cand_w.1), custom_call_target="tpu_custom_call" | custom-call | tf_op jit(solution)/shard_map/pallas_call | solution.py:453
  74.7 2.3 %copy.10 = f32[64,8,512]{2,1,0:T(8,128)} copy(f32[64,8,512]{2,1,0:T(8,128)} %get-tuple-element.8) | data formatting | bytes 2097152

commit v2 on v1

--- a/solution.py
+++ b/solution.py
@@ -29,9 +29,10 @@
 
 def kernel(
     traj, init, dgate, dcand, gate_w, cand_w, out, res,
-    A, W, acc, trv, dgv, dcv, first_in, first, maps, sib_map, y_maps, x_maps, z_sums,
+    A, W, acc, trv, dgv, dcv, first_in, first, maps, sib_map, y_maps, x_maps,
+    sums, z_sums, plane_sums,
     local_sem, bound_s, bound_r, a_s, a_r, wz_s, wz_r, p1_s, p1_r, p1b_s, p1b_r,
-    p2_s, p2_r, p2b_s, p2b_r, d_s, d_r, m_s, m_r,
+    p2_s, p2_r, p2b_s, p2b_r, d_s, d_r, m_s, m_r, q_s, q_r,
 ):
     z, x, y, c = (lax.axis_index(a) for a in AXES)
     t = (x * NY + y) * NC + c
@@ -48,6 +49,9 @@
 
     def at_y(d):
         return (z, x, lax.rem(y + d + NY, NY), c)
+
+    def at_plane(k):
+        return (z, lax.rem(x + k // NY, NX), lax.rem(y + k % NY, NY), c)
 
     sibling = (z, x, y, 1 - c)
     me1 = x * (1 - c) + y * c
@@ -78,8 +82,7 @@
     barrier = pltpu.get_barrier_semaphore()
     peers = (
         [at_z(d) for d in range(1, NZ)]
-        + [at_x(d) for d in range(1, NX)]
-        + [at_y(d) for d in range(1, NY)]
+        + [at_plane(k) for k in range(1, NX * NY)]
         + [sibling, at_time(t + 1), at_time(t - 1)]
     )
     for peer in peers:
@@ -102,30 +105,30 @@
 
     for load in loads[1:]:
         load.start()
+    pl.semaphore_wait(barrier, len(peers))
+
+    def spread(ref):
+        for d in range(1, NZ):
+            to = at_z(d)
+            remote(ref.at[own_rows, columns(to[0])], W.at[c, mine, z], wz_s, wz_r, to).start()
+
+    @pl.when(c == 0)
+    def _():
+        spread(gate_w)
+
+    @pl.when(c == 1)
+    def _():
+        spread(cand_w)
+
     loads[0].wait()
+    boundary = remote(trv.at[STEPS - 1], first_in.at[1], bound_s, bound_r, at_time(t + 1))
+    boundary.start()
     for q in range(1, PIECES):
         A[z, q] = (
             trv[q * PIECE_STEPS - 1 : (q + 1) * PIECE_STEPS - 1]
             .reshape(PIECE, WIDTH)
             .astype(jnp.bfloat16)
         )
-    pl.semaphore_wait(barrier, len(peers))
-
-    boundary = remote(trv.at[STEPS - 1], first_in.at[1], bound_s, bound_r, at_time(t + 1))
-    boundary.start()
-
-    def spread(ref):
-        for d in range(1, NZ):
-            to = at_z(d)
-            remote(ref.at[own_rows, columns(to[0])], W.at[c, mine, z], wz_s, wz_r, to).start()
-
-    @pl.when(c == 0)
-    def _():
-        spread(gate_w)
-
-    @pl.when(c == 1)
-    def _():
-        spread(cand_w)
 
     def a_copy(way, i):
         d, q = arrivals(way)[i]
@@ -146,9 +149,6 @@
             if (d + 1, q) in arrivals(way):
                 a_copy(way, arrivals(way).index((d + 1, q))).start()
 
-    for i in range(3):
-        for way in (0, 1):
-            a_copy(way, i).start()
     boundary.wait_recv()
     loads[3].wait()
     first[...] = jnp.where(t == 0, first_in[0], first_in[1])
@@ -157,6 +157,9 @@
         .reshape(PIECE, WIDTH)
         .astype(jnp.bfloat16)
     )
+    for i in range(3):
+        for way in (0, 1):
+            a_copy(way, i).start()
 
     def whole(d2, d1):
         return W.at[c, share(d2, d1)]
@@ -351,61 +354,64 @@
     for q in range(1, PIECES):
         prod, state = found[q][0] * prod, found[q][0] * state + found[q][1]
 
-    def store_map(ref, prod, state, square):
-        for k in range(TILES):
-            ref[k] = prod[:, k * 128 : (k + 1) * 128]
-            ref[TILES + k] = state[:, k * 128 : (k + 1) * 128]
-        ref[2 * TILES] = square
-
-    def load_map(ref):
-        return (
-            jnp.concatenate([ref[k] for k in range(TILES)], axis=1),
-            jnp.concatenate([ref[TILES + k] for k in range(TILES)], axis=1),
-            ref[2 * TILES],
-        )
+    def store_map(ref, prod, state):
+        ref[0], ref[1] = prod, state
 
     square = squares[:, :128]
     for k in range(1, TILES):
         square = square + squares[:, k * 128 : (k + 1) * 128]
-    store_map(maps.at[0], prod, state, square)
+    square = jnp.sum(square, axis=0, keepdims=True)
+    store_map(maps.at[0], prod, state)
+    sums[0] = square
     sib = remote(maps.at[0], sib_map, m_s.at[0], m_r.at[0], sibling)
+    sib_sum = remote(sums.at[0], sums.at[3], q_s.at[0], q_r.at[0], sibling)
     sib.start()
+    sib_sum.start()
     sib.wait_recv()
-    s_prod, s_state, s_square = load_map(sib_map)
+    s_prod, s_state = sib_map[0], sib_map[1]
     odd = c == 1
     e_prod, e_state = jnp.where(odd, s_prod, prod), jnp.where(odd, s_state, state)
     l_prod, l_state = jnp.where(odd, prod, s_prod), jnp.where(odd, state, s_state)
-    store_map(maps.at[1], l_prod * e_prod, l_prod * e_state + l_state, square + s_square)
+    store_map(maps.at[1], l_prod * e_prod, l_prod * e_state + l_state)
 
     def exchange(k, slots, count, index, peer):
         for d in range(1, count):
             remote(maps.at[k], slots.at[index], m_s.at[k], m_r.at[k], peer(d)).start()
         slots[index] = maps[k]
+
+    def exchanged(k, slots, count, peer):
         three = slots.at[pl.ds(0, count - 1)]
         remote(three, three, m_s.at[k], m_r.at[k], peer(1)).wait_recv()
 
     exchange(1, y_maps, NY, y, at_y)
-    total = load_map(y_maps.at[0])
+    sib_sum.wait_recv()
+    sums[1] = square + sums[3]
+    for d in range(1, NZ):
+        remote(sums.at[1], z_sums.at[z], q_s.at[1], q_r.at[1], at_z(d)).start()
+    z_sums[z] = sums[1]
+    exchanged(1, y_maps, NY, at_y)
+    prod, state = y_maps[0, 0], y_maps[0, 1]
     for k in range(1, NY):
-        n_prod, n_state, n_square = load_map(y_maps.at[k])
-        total = (n_prod * total[0], n_prod * total[1] + n_state, total[2] + n_square)
-    store_map(maps.at[2], *total)
+        prod, state = y_maps[k, 0] * prod, y_maps[k, 0] * state + y_maps[k, 1]
+    store_map(maps.at[2], prod, state)
     exchange(2, x_maps, NX, x, at_x)
-
-    square = x_maps[0, 2 * TILES]
-    for k in range(1, NX):
-        square = square + x_maps[k, 2 * TILES]
-    maps[3, 0] = square
-    for d in range(1, NZ):
-        remote(maps.at[3, 0], z_sums.at[z], m_s.at[3], m_r.at[3], at_z(d)).start()
+    seven_sums = z_sums.at[pl.ds(0, NZ - 1)]
+    remote(seven_sums, seven_sums, q_s.at[1], q_r.at[1], at_z(1)).wait_recv()
+    square = z_sums[0]
+    for k in range(1, NZ):
+        square = square + z_sums[k]
+    sums[2] = square
+    plane = x * NY + y
+    for k in range(1, NX * NY):
+        remote(sums.at[2], plane_sums.at[plane], q_s.at[2], q_r.at[2], at_plane(k)).start()
+    plane_sums[plane] = square
+    exchanged(2, x_maps, NX, at_x)
 
     value = first_in[0]
     for k in range(NX - 1):
-        n_prod, n_state, _ = load_map(x_maps.at[k])
-        value = jnp.where(k < x, n_prod * value + n_state, value)
+        value = jnp.where(k < x, x_maps[k, 0] * value + x_maps[k, 1], value)
     for k in range(NY - 1):
-        n_prod, n_state, _ = load_map(y_maps.at[k])
-        value = jnp.where(k < y, n_prod * value + n_state, value)
+        value = jnp.where(k < y, y_maps[k, 0] * value + y_maps[k, 1], value)
     value = jnp.where(odd, s_prod * value + s_state, value)
 
     def run(i, value):
@@ -418,14 +424,12 @@
 
     lax.fori_loop(0, STEPS // 4, run, value)
 
-    z_sums[z] = square
-    seven_sums = z_sums.at[pl.ds(0, NZ - 1)]
-    remote(seven_sums, seven_sums, m_s.at[3], m_r.at[3], at_z(1)).wait_recv()
-    square = z_sums[0]
-    for k in range(1, NZ):
-        square = square + z_sums[k]
-    whole_sum = jnp.sum(jnp.sum(square, axis=0, keepdims=True), axis=1, keepdims=True)
-    res[...] = jnp.sqrt(whole_sum / ENTRIES + 1e-06)
+    fifteen = plane_sums.at[pl.ds(0, NX * NY - 1)]
+    remote(fifteen, fifteen, q_s.at[2], q_r.at[2], at_plane(1)).wait_recv()
+    square = plane_sums[0]
+    for k in range(1, NX * NY):
+        square = square + plane_sums[k]
+    res[...] = jnp.sqrt(jnp.sum(square, axis=1, keepdims=True) / ENTRIES + 1e-06)
 
     boundary.wait_send()
     remote(seven, seven, wz_s, wz_r, at_z(1)).wait_send()
@@ -441,20 +445,22 @@
     ours = W.at[c]
     remote(ours, ours, d_s, d_r, sibling).wait_send()
     sib.wait_send()
+    sib_sum.wait_send()
     for k, slots in ((1, y_maps), (2, x_maps)):
         three = slots.at[pl.ds(0, 3)]
         remote(three, three, m_s.at[k], m_r.at[k], at_y(1)).wait_send()
-    remote(seven_sums, seven_sums, m_s.at[3], m_r.at[3], at_z(1)).wait_send()
+    remote(seven_sums, seven_sums, q_s.at[1], q_r.at[1], at_z(1)).wait_send()
+    remote(fifteen, fifteen, q_s.at[2], q_r.at[2], at_plane(1)).wait_send()
 
 
 def local(trajectory, initial, drive_gate, drive_candidate, gate_weight, candidate_weight):
     dma = pltpu.SemaphoreType.DMA
-    tiles = (2 * TILES + 1, BATCH, 128)
+    pair = (2, BATCH, WIDTH)
     states, residual = pl.pallas_call(
         kernel,
         out_shape=(
-            jax.ShapeDtypeStruct((STEPS, BATCH, WIDTH), jnp.float32),
-            jax.ShapeDtypeStruct((1, 1), jnp.float32),
+            pltpu.VMEM((STEPS, BATCH, WIDTH), jnp.float32),
+            pltpu.VMEM((1, 1), jnp.float32),
         ),
         in_specs=[pl.BlockSpec(memory_space=pl.ANY)] * 6,
         out_specs=(
@@ -470,11 +476,13 @@
             pltpu.VMEM((STEPS, BATCH, WIDTH), jnp.bfloat16),
             pltpu.VMEM((2, BATCH, WIDTH), jnp.float32),
             pltpu.VMEM((BATCH, WIDTH), jnp.float32),
-            pltpu.VMEM((4, *tiles), jnp.float32),
-            pltpu.VMEM(tiles, jnp.float32),
-            pltpu.VMEM((NY, *tiles), jnp.float32),
-            pltpu.VMEM((NX, *tiles), jnp.float32),
-            pltpu.VMEM((NZ, BATCH, 128), jnp.float32),
+            pltpu.VMEM((3, *pair), jnp.float32),
+            pltpu.VMEM(pair, jnp.float32),
+            pltpu.VMEM((NY, *pair), jnp.float32),
+            pltpu.VMEM((NX, *pair), jnp.float32),
+            pltpu.VMEM((4, 1, 128), jnp.float32),
+            pltpu.VMEM((NZ, 1, 128), jnp.float32),
+            pltpu.VMEM((NX * NY, 1, 128), jnp.float32),
             dma((5,)),
             dma,
             dma,
@@ -492,8 +500,10 @@
             dma((4,)),
             dma,
             dma,
-            dma((4,)),
-            dma((4,)),
+            dma((3,)),
+            dma((3,)),
+            dma((3,)),
+            dma((3,)),
         ],
         compiler_params=pltpu.CompilerParams(collective_id=0, has_side_effects=True),
     )(trajectory, initial, drive_gate, drive_candidate, gate_weight, candidate_weight)

time: 78.8 us -> 73 us (0.926)
  Pallas kernels: 74.1 us -> 70.2 us
  local copies, waits for them, and re-layouts: 2.26 us -> 0.97 us
    pallas_call x1, Pallas kernels: 74.1 us -> 70.2 us  [local(): pl.pallas_call(kernel, out_shape=(pltpu.VMEM((STEPS, BATCH, WIDTH), jnp.f...]
    unnamed x1, local copies, waits for them, and re-layouts: 2.26 us -> 0.97 us
where the time goes in v2:
time: 73 us; the launch traced here: 72.9 us
  Pallas kernels  70.2 us (96%)
  between operations  1.8 us (2%)
  local copies, waits for them, and re-layouts  0.97 us (1%)
    pallas_call x1, Pallas kernels, local(): pl.pallas_call(kernel, out_shape=(pltpu.VMEM((STEPS, BATCH, WIDTH), jnp.f...  70.2 us

profile of v2, /device:TPU:1, one launch (start us, length us, event | category | flops | bytes accessed | tf_op | source)
XLA Modules:
  0.0 72.9 jit_solution(14480250453825314809)
XLA Ops:
  0.6 70.2 %shard_map.77 = (f32[64,8,512]{2,1,0:T(8,128)S(1)}, f32[1,1]{1,0:T(1,128)S(1)}) custom-call(f32[64,8,512]{2,1,0:T(8,128)} %traj.1, f32[8,512]{1,0:T(8,128)} %init.1, bf16[64,8,512]{2,1,0:T(8,128)(2,1)} %dgate.1, bf16[64,8,512]{2,1,0:T(8,128)(2,1)} %dcand.1, bf16[512,4096]{1,0:T(8,128)(2,1)} %gate_w.1, bf16[512,4096]{1,0:T(8,128)(2,1)} %cand_w.1), custom_call_target="tpu_custom_call" | custom-call | tf_op jit(solution)/shard_map/pallas_call | solution.py:459
  70.8 1.0 %copy.10 = f32[64,8,512]{2,1,0:T(8,128)} copy(f32[64,8,512]{2,1,0:T(8,128)S(1)} %get-tuple-element.6) | data formatting | bytes 2097152
